TPU v7x, 32 devices: a whole 2x2x4 slice. The times are simulated.
32 devices in a mesh: tables: 8 (over z, y), cells: 4 (over x, core).
Axes of the slice: x: 2, y: 2, z: 4, core: 2. Of those that a mesh axis runs over, the one named last changes fastest.
Arguments:
- cells_in: bfloat16 [8, 128, 112, 192], P('tables', 'cells'), may hold values from -6 to 6
- train_count: int32 [8], P('tables'), may hold values from 32 to 96
- feat_count: int32 [8], P('tables'), may hold values from 28 to 112
- feat_qkv: bfloat16 [192, 576], replicated, may hold values from -2 to 2
- feat_proj: bfloat16 [192, 192], replicated, may hold values from -2 to 2
- row_qkv: bfloat16 [192, 576], replicated, may hold values from -2 to 2
- row_proj: bfloat16 [192, 192], replicated, may hold values from -0.4375 to 0.4375
- w_in: bfloat16 [192, 768], replicated, may hold values from -0.4375 to 0.4375
- w_out: bfloat16 [768, 192], replicated, may hold values from -0.21875 to 0.21875
- cotangent: bfloat16 [8, 128, 112, 192], P('tables', 'cells'), may hold values from -6 to 6
Outputs:
- cells_out: bfloat16 [8, 128, 112, 192], P('tables', 'cells')
- grad_in: float32 [192, 768], P(None, ('tables', 'cells'))
- grad_out: float32 [768, 192], P(('tables', 'cells'))
All inputs are finite; a program needn't handle non-finite values.
Results may differ from a plain program's by a relative error of at most 0.018.
Values may be sent and summed in bfloat16 or wider, within the bound.
A program may use at most 128 MiB of HBM per device.

v0:
```python
import math

import jax
import jax.numpy as jnp
from jax import lax
from jax.experimental import pallas as pl
from jax.experimental.pallas import tpu as pltpu
from jax.sharding import PartitionSpec as P

HEADS = 6
HEAD_DIM = 32
NEG = -1e30
UNROLL = 8
GROUP = 4
LOG2E = math.log2(math.e)
SCALE = LOG2E / math.sqrt(HEAD_DIM)
AXES = ("tables", "cells")
F32 = jnp.float32
BF16 = jnp.bfloat16


def dot(a, b, ca, cb):
    return lax.dot_general(a, b, (((ca,), (cb,)), ((), ())), preferred_element_type=F32)


def layer_norm(values, axis):
    mean = jnp.mean(values, axis=axis, keepdims=True)
    centred = values - mean
    var = jnp.mean(centred * centred, axis=axis, keepdims=True)
    return centred * lax.rsqrt(var + 1e-05)


def attend(packs, limit):
    width, n = packs[0].shape[0] // 3, packs[0].shape[1]
    keep = lax.broadcasted_iota(jnp.int32, (n, 1), 0) < limit
    step = n if n <= 128 else 128
    jobs = [(i, h, q0) for i in range(len(packs)) for h in range(HEADS) for q0 in range(0, n, step)]
    scores, probs, outs = [], [], []
    for i, h, q0 in jobs:
        lo = h * HEAD_DIM
        keys = packs[i][width + lo : width + lo + HEAD_DIM]
        query = packs[i][lo : lo + HEAD_DIM, q0 : q0 + step]
        scores.append(dot(keys, query, 0, 0))
    for score in scores:
        score = jnp.where(keep, score, NEG)
        prob = jnp.exp2((score - jnp.max(score, axis=0, keepdims=True)) * SCALE)
        probs.append((prob.astype(BF16), 1.0 / jnp.sum(prob, axis=0, keepdims=True)))
    for (i, h, q0), (prob, inverse) in zip(jobs, probs):
        lo = 2 * width + h * HEAD_DIM
        outs.append((dot(packs[i][lo : lo + HEAD_DIM], prob, 1, 0), inverse))
    outs = [(out * inverse).astype(BF16) for out, inverse in outs]
    blocks = n // step
    result = []
    for i in range(len(packs)):
        heads = []
        for h in range(HEADS):
            at = (i * HEADS + h) * blocks
            cols = outs[at : at + blocks]
            heads.append(cols[0] if blocks == 1 else jnp.concatenate(cols, axis=1))
        result.append(jnp.concatenate(heads, axis=0))
    return result


def feature_kernel(limit_ref, x_ref, wn_ref, pn_ref, o_ref, lo_ref, hi_ref, w_ref, p_ref):
    rows, width, feats = x_ref.shape
    limit = limit_ref[0]

    @pl.when(pl.program_id(0) == 0)
    def _():
        w_ref[...] = wn_ref[...].T
        p_ref[...] = pn_ref[...].T

    unroll = UNROLL if rows % UNROLL == 0 else 1

    def body(i, carry):
        spots = [i * unroll + k for k in range(unroll)]
        cells = [x_ref[r] for r in spots]
        packs = [dot(w_ref[...], x, 1, 0).astype(BF16) for x in cells]
        attended = attend(packs, limit)
        mixed = [dot(p_ref[...], a, 1, 0) for a in attended]
        for r, x, m in zip(spots, cells, mixed):
            y = layer_norm(x.astype(F32) + m, 0)
            spot = pl.ds(r, feats, stride=rows)
            lo_ref[spot, :] = y[:128].T
            hi_ref[spot, :] = jnp.concatenate([y[128:], jnp.zeros((256 - width, feats), F32)], axis=0).T
        return carry

    lax.fori_loop(0, rows // unroll, body, 0)
    o_ref[:, :, :128] = lo_ref[...].reshape(feats, rows, 128).astype(BF16)
    o_ref[:, :, 128:] = hi_ref[...].reshape(feats, rows, 128)[:, :, : width - 128].astype(BF16)


def row_kernel(limit_ref, x_ref, wn_ref, p_ref, o_ref, w_ref):
    groups, block, rows, width = x_ref.shape
    limit = limit_ref[0]

    @pl.when(pl.program_id(0) == 0)
    def _():
        w_ref[...] = wn_ref[...].T


    unroll = block

    def body(i, carry):
        spots = [i * unroll + k for k in range(unroll)]
        cells = [x_ref[:, f].reshape(groups * rows, width) for f in spots]
        packs = [dot(w_ref[...], x, 1, 1).astype(BF16) for x in cells]
        attended = attend(packs, limit)
        mixed = [dot(a, p_ref[...], 0, 0) for a in attended]
        for f, x, m in zip(spots, cells, mixed):
            y = layer_norm(x.astype(F32) + m, -1)
            o_ref[:, f] = y.astype(BF16).reshape(groups, rows, width)
        return carry

    lax.fori_loop(0, block // unroll, body, 0)


def gelu_pair(x):
    bell = jnp.exp2(x * x * (-0.5 * LOG2E))
    t = 1.0 / (1.0 + (0.3275911 * math.sqrt(0.5)) * jnp.abs(x))
    poly = 0.5 * 1.061405429 * t + (0.5 * -1.453152027)
    poly = poly * t + (0.5 * 1.421413741)
    poly = poly * t + (0.5 * -0.284496736)
    poly = poly * t + (0.5 * 0.254829592)
    tail = poly * t * bell
    cdf = jnp.where(x < 0, tail, 1.0 - tail)
    return x * cdf, cdf + x * bell * (1.0 / math.sqrt(2.0 * math.pi))


def dense_kernel(factor, x_ref, c_ref, wi_ref, wo_ref, o_ref, gi_ref, go_ref, lo_ref, hi_ref, ai_ref, ao_ref):
    feats, rows, width = x_ref.shape
    cells = feats * rows
    step = pl.program_id(0)

    @pl.when(step == 0)
    def _():
        ai_ref[...] = jnp.zeros_like(ai_ref)
        ao_ref[...] = jnp.zeros_like(ao_ref)

    lo_ref[...] = x_ref[:, :, :128].astype(F32).reshape(cells, 128)
    hi_ref[:, : width - 128] = x_ref[:, :, 128:].astype(F32).reshape(cells, width - 128)
    group = GROUP if rows % GROUP == 0 else 1

    def body(i, carry):
        spots = [i * group + k for k in range(group)]
        parts, cots = [], []
        for r in spots:
            spot = pl.ds(r, feats, stride=rows)
            parts.append(jnp.concatenate([lo_ref[spot, :], hi_ref[spot, :][:, : width - 128]], axis=1).astype(BF16))
            cots.append(c_ref[r].T)
        normed = jnp.concatenate(parts, axis=0)
        cot = jnp.concatenate(cots, axis=0)
        act, slope = gelu_pair(dot(normed, wi_ref[...], 1, 0))
        act = act.astype(BF16)
        dpre = (dot(cot, wo_ref[...], 1, 0) * slope).astype(BF16)
        out = normed.astype(F32) + dot(act, wo_ref[...], 1, 1)
        for k, r in enumerate(spots):
            o_ref[r] = out[k * feats : (k + 1) * feats].T.astype(BF16)
        ai_ref[...] += dot(normed, dpre, 0, 0)
        ao_ref[...] += dot(cot, act, 0, 0)
        return carry

    lax.fori_loop(0, rows // group, body, 0)

    @pl.when(step == pl.num_programs(0) - 1)
    def _():
        gi_ref[...] = (ai_ref[...] * factor).T.astype(BF16)
        go_ref[...] = (ao_ref[...] * factor).T.astype(BF16)


def whole_spec(array):
    return pl.BlockSpec(array.shape, lambda i: (0,) * array.ndim)


def divisor(n, most):
    return max(k for k in range(1, most + 1) if n % k == 0)


def run_feature(limit, block, w_qkv, w_proj):
    rows, width, feats = block.shape
    part = 16 if rows % 16 == 0 else rows
    return pl.pallas_call(
        feature_kernel,
        grid=(rows // part,),
        out_shape=jax.ShapeDtypeStruct((feats, rows, width), BF16),
        in_specs=[
            pl.BlockSpec(memory_space=pltpu.SMEM),
            pl.BlockSpec((part, width, feats), lambda i: (i, 0, 0)),
            whole_spec(w_qkv),
            whole_spec(w_proj),
        ],
        out_specs=pl.BlockSpec((feats, part, width), lambda i: (0, i, 0)),
        scratch_shapes=[pltpu.VMEM((feats * part, 128), F32)] * 2
        + [pltpu.VMEM(w_qkv.shape[::-1], BF16), pltpu.VMEM(w_proj.shape[::-1], BF16)],
        cost_estimate=pl.CostEstimate(flops=4 * 10**9, bytes_accessed=4 * 10**6, transcendentals=0),
        name="feature",
    )(limit, block, w_qkv, w_proj)


def run_row(limit, columns, w_qkv, w_proj):
    groups, feats, rows, width = columns.shape
    part = divisor(feats, 7 if groups * rows <= 128 else 1)
    spec = pl.BlockSpec((groups, part, rows, width), lambda i: (0, i, 0, 0))
    return pl.pallas_call(
        row_kernel,
        grid=(feats // part,),
        out_shape=jax.ShapeDtypeStruct(columns.shape, BF16),
        in_specs=[pl.BlockSpec(memory_space=pltpu.SMEM), spec, whole_spec(w_qkv), whole_spec(w_proj)],
        out_specs=spec,
        scratch_shapes=[pltpu.VMEM(w_qkv.shape[::-1], BF16)],
        cost_estimate=pl.CostEstimate(flops=4 * 10**9, bytes_accessed=4 * 10**6, transcendentals=0),
        name="row",
    )(limit, columns, w_qkv, w_proj)


def run_dense(factor, normed, cot, w_in, w_out):
    feats, rows, width = normed.shape
    hidden = w_in.shape[1]
    part = 8 if rows % 8 == 0 else rows
    natural = pl.BlockSpec((part, width, feats), lambda i: (i, 0, 0))
    grad = pl.BlockSpec((hidden, width), lambda i: (0, 0))
    return pl.pallas_call(
        lambda *refs: dense_kernel(factor, *refs),
        grid=(rows // part,),
        out_shape=[
            jax.ShapeDtypeStruct((rows, width, feats), BF16),
            jax.ShapeDtypeStruct((hidden, width), BF16),
            jax.ShapeDtypeStruct((hidden, width), BF16),
        ],
        in_specs=[
            pl.BlockSpec((feats, part, width), lambda i: (0, i, 0)),
            natural,
            whole_spec(w_in),
            whole_spec(w_out),
        ],
        out_specs=[natural, grad, grad],
        scratch_shapes=[pltpu.VMEM((part * feats, 128), F32)] * 2 + [pltpu.VMEM((width, hidden), F32)] * 2,
        cost_estimate=pl.CostEstimate(flops=8 * 10**9, bytes_accessed=6 * 10**6, transcendentals=0),
        name="dense",
    )(normed, cot, w_in, w_out)


def exchange_kernel(axes, sizes, x_ref, o_ref, own_ref, own_sem, send_sem, recv_sem):
    count = math.prod(sizes)
    me = 0
    for axis, size in zip(axes, sizes):
        me = me * size + lax.axis_index(axis)

    def target(k):
        peer = lax.rem(me + k, count)
        if len(axes) == 1:
            return peer, {axes[0]: peer}
        return peer, {axes[0]: lax.div(peer, sizes[1]), axes[1]: lax.rem(peer, sizes[1])}

    def copy(k):
        peer, device = target(k)
        return pltpu.make_async_remote_copy(
            src_ref=x_ref.at[peer],
            dst_ref=o_ref.at[me],
            send_sem=send_sem.at[k],
            recv_sem=recv_sem.at[k],
            device_id=device,
            device_id_type=pl.DeviceIdType.MESH,
        )

    barrier = pltpu.get_barrier_semaphore()

    def greet(k, carry):
        pl.semaphore_signal(barrier, inc=1, device_id=target(k)[1], device_id_type=pl.DeviceIdType.MESH)
        return carry

    def start(k, carry):
        copy(k).start()
        return carry

    def finish(k, carry):
        copy(k).wait()
        return carry

    load = pltpu.make_async_copy(x_ref.at[me], own_ref, own_sem.at[0])
    load.start()
    lax.fori_loop(1, count, greet, 0)
    pl.semaphore_wait(barrier, count - 1)
    lax.fori_loop(1, count, start, 0)
    load.wait()
    store = pltpu.make_async_copy(own_ref, o_ref.at[me], own_sem.at[1])
    store.start()
    lax.fori_loop(1, count, finish, 0)
    store.wait()


def exchange(array, axes, ident):
    sizes = [lax.axis_size(axis) for axis in axes]
    return pl.pallas_call(
        lambda *refs: exchange_kernel(axes, sizes, *refs),
        out_shape=jax.ShapeDtypeStruct(array.shape, array.dtype),
        in_specs=[pl.BlockSpec(memory_space=pl.ANY)],
        out_specs=pl.BlockSpec(memory_space=pl.ANY),
        scratch_shapes=[
            pltpu.VMEM(array.shape[1:], array.dtype),
            pltpu.SemaphoreType.DMA((2,)),
            pltpu.SemaphoreType.DMA((array.shape[0],)),
            pltpu.SemaphoreType.DMA((array.shape[0],)),
        ],
        compiler_params=pltpu.CompilerParams(collective_id=ident, has_side_effects=True),
        name="exchange%d" % ident,
    )(array)


def per_device(
    cells_in, train_count, feat_count, feat_qkv, feat_proj, row_qkv, row_proj, w_in, w_out, cotangent
):
    block = cells_in[0]
    rows, feats, width = block.shape
    groups = lax.axis_size("cells")
    devices = groups * lax.axis_size("tables")
    mid = run_feature(feat_count, jnp.swapaxes(block, 1, 2), feat_qkv, feat_proj)
    columns = mid.reshape(groups, feats // groups, rows, width)
    columns = exchange(columns, ("cells",), 0)
    done = run_row(train_count, columns, row_qkv, row_proj)
    normed = exchange(done, ("cells",), 1)
    factor = 1.0 / math.sqrt(devices * rows * feats)
    output, part_in, part_out = run_dense(
        factor, normed.reshape(feats, rows, width), jnp.swapaxes(cotangent[0], 1, 2), w_in, w_out.T
    )
    own = part_in.shape[0] // devices
    sends = jnp.concatenate(
        [part_in.reshape(devices, own, width), part_out.reshape(devices, own, width)], axis=1
    )
    got = exchange(sends, AXES, 2)
    total = jnp.sum(got.astype(F32), axis=0)
    return jnp.swapaxes(output, 1, 2)[None], total[:own].T, total[own:]


def solution(mesh):
    return jax.shard_map(
        per_device,
        mesh=mesh,
        in_specs=(
            P("tables", "cells", None, None),
            P("tables"),
            P("tables"),
            P(),
            P(),
            P(),
            P(),
            P(),
            P(),
            P("tables", "cells", None, None),
        ),
        out_specs=(
            P("tables", "cells", None, None),
            P(None, ("tables", "cells")),
            P(("tables", "cells"), None),
        ),
        check_vma=False,
    )
```

profile of v0, /device:TPU:8, one launch (start us, length us, event | category | flops | bytes accessed | tf_op | source)
XLA Modules:
  0.0 114.7 jit_solution(6310029254567360137)
XLA Ops:
  1.9 12.9 %feature.1 = bf16[112,32,192]{2,1,0:T(8,128)(2,1)} custom-call(s32[1]{0:T(128)S(6)} %copy.14.limit_ref, bf16[32,192,112]{2,1,0:T(8,128)(2,1)} %bitcast.20, bf16[192,576]{1,0:T(8,128)(2,1)} %wn_ref.2, bf16[192,192]{1,0:T(8,128)(2,1)} %pn_ref.1), custom_call_target="tpu_custom_call" | custom-call | flops 4000000000 | bytes 4000000 | tf_op jit(solution)/shard_map/feature/pallas_call | solution.py:182
  14.8 22.1 %exchange0.1.x_ref = bf16[4,28,32,192]{3,2,1,0:T(8,128)(2,1)} custom-call(bf16[4,28,32,192]{3,2,1,0:T(8,128)(2,1)} %bitcast.17), custom_call_target="tpu_custom_call" | custom-call | tf_op jit(solution)/shard_map/exchange0/pallas_call | solution.py:294
  36.9 10.2 %row.1.refs_0_ = bf16[4,28,32,192]{3,2,1,0:T(8,128)(2,1)} custom-call(s32[1]{0:T(128)S(6)} %copy.13.limit_ref, bf16[4,28,32,192]{3,2,1,0:T(8,128)(2,1)} %exchange0.1.x_ref, bf16[192,576]{1,0:T(8,128)(2,1)} %wn_ref.3, bf16[192,192]{1,0:T(8,128)(2,1)} %p_ref.1), custom_call_target="tpu_custom_call" | custom-call | flops 4000000000 | bytes 4000000 | tf_op jit(solution)/shard_map/row/pallas_call | solution.py:204
  47.1 22.5 %exchange1.1 = bf16[4,28,32,192]{3,2,1,0:T(8,128)(2,1)} custom-call(bf16[4,28,32,192]{3,2,1,0:T(8,128)(2,1)} %row.1.refs_0_), custom_call_target="tpu_custom_call" | custom-call | tf_op jit(solution)/shard_map/exchange1/pallas_call | solution.py:294
  69.6 18.0 %dense.1 = (bf16[32,192,112]{2,1,0:T(8,128)(2,1)}, bf16[768,192]{1,0:T(8,128)(2,1)}, bf16[768,192]{1,0:T(8,128)(2,1)}) custom-call(bf16[112,32,192]{2,1,0:T(8,128)(2,1)} %bitcast.16, bf16[32,192,112]{2,1,0:T(8,128)(2,1)} %bitcast.21, bf16[192,768]{1,0:T(8,128)(2,1)} %refs_2_.1, bf16[192,768]{1,0:T(8,128)(2,1)} %bitcast.22), custom_call_target="tpu_custom_call" | custom-call | flops 8000000000 | bytes 6000000 | tf_op jit(solution)/shard_map/dense/pallas_call | solution.py:222
  87.5 2.1 %pad_maximum_fusion.refs_0_ = bf16[32,48,192]{2,1,0:T(8,128)(2,1)} fusion(bf16[32,24,192]{2,1,0:T(8,128)(2,1)} %bitcast.19, bf16[32,24,192]{2,1,0:T(8,128)(2,1)} %bitcast.18), kind=kLoop, calls=%fused_computation.1 | loop fusion | flops 1179648 | bytes 1179648 | tf_op jit(solution)/shard_map/concatenate | solution.py:327
  89.7 23.1 %exchange2.1 = bf16[32,48,192]{2,1,0:T(8,128)(2,1)} custom-call(bf16[32,48,192]{2,1,0:T(8,128)(2,1)} %pad_maximum_fusion.refs_0_), custom_call_target="tpu_custom_call" | custom-call | tf_op jit(solution)/shard_map/exchange2/pallas_call | solution.py:294
  112.8 1.3 %convert_reduce_fusion = f32[48,192]{1,0:T(8,128)S(1)} fusion(bf16[32,48,192]{2,1,0:T(8,128)(2,1)} %exchange2.1), kind=kLoop, calls=%fused_computation | loop fusion | flops 580608 | bytes 626688 | tf_op jit(solution)/shard_map/reduce_sum | solution.py:331
  114.0 0.6 fusion
where the time goes:
time: 116 us; the launch traced here: 115 us
  Pallas kernels  109 us (94%)
  other arithmetic  3.41 us (3%)
  between operations  1.95 us (2%)
    pallas_call x3, Pallas kernels, exchange(): pl.pallas_call(lambda *refs: exchange_kernel(axes, sizes, *refs), out_sha...  67.7 us
    pallas_call x1, Pallas kernels, run_dense(): pl.pallas_call(lambda *refs: dense_kernel(factor, *refs), grid=(rows // p...  18 us
    pallas_call x1, Pallas kernels, run_feature(): pl.pallas_call(feature_kernel, grid=(rows // part,), out_shape=jax.ShapeD...  12.9 us
    pallas_call x1, Pallas kernels, run_row(): pl.pallas_call(row_kernel, grid=(feats // part,), out_shape=jax.ShapeDtyp...  10.2 us

commit v1 on v0

v1 whole, which is shorter than its diff:
```python
import math

import jax
import jax.numpy as jnp
from jax import lax
from jax.experimental import pallas as pl
from jax.experimental.pallas import tpu as pltpu
from jax.sharding import PartitionSpec as P

HEADS = 6
HEAD_DIM = 32
NEG = -1e30
LOG2E = math.log2(math.e)
SCALE = LOG2E / math.sqrt(HEAD_DIM)
AXES = ("tables", "cells")
F32 = jnp.float32
BF16 = jnp.bfloat16


def dot(a, b, ca, cb):
    return lax.dot_general(a, b, (((ca,), (cb,)), ((), ())), preferred_element_type=F32)


def layer_norm(values, axis):
    mean = jnp.mean(values, axis=axis, keepdims=True)
    centred = values - mean
    var = jnp.mean(centred * centred, axis=axis, keepdims=True)
    return centred * lax.rsqrt(var + 1e-05)


def attend(packs, limit, most, least):
    width, n = packs[0].shape[0] // 3, packs[0].shape[1]
    open_rows = least // 8 * 8
    keep = lax.broadcasted_iota(jnp.int32, (most - open_rows, 1), 0) + open_rows < limit
    step = n if n <= 128 else 128
    jobs = [(i, h, q0) for i in range(len(packs)) for h in range(HEADS) for q0 in range(0, n, step)]
    scores, probs, outs = [], [], []
    for i, h, q0 in jobs:
        lo = h * HEAD_DIM
        keys = packs[i][width + lo : width + lo + HEAD_DIM, :most]
        query = packs[i][lo : lo + HEAD_DIM, q0 : q0 + step]
        scores.append(dot(keys, query, 0, 0))
    for score in scores:
        tail = jnp.where(keep, score[open_rows:], NEG)
        score = jnp.concatenate([score[:open_rows], tail], axis=0) if open_rows else tail
        prob = jnp.exp2((score - jnp.max(score, axis=0, keepdims=True)) * SCALE)
        probs.append((prob.astype(BF16), 1.0 / jnp.sum(prob, axis=0, keepdims=True)))
    for (i, h, q0), (prob, inverse) in zip(jobs, probs):
        lo = 2 * width + h * HEAD_DIM
        outs.append((dot(packs[i][lo : lo + HEAD_DIM, :most], prob, 1, 0), inverse))
    outs = [(out * inverse).astype(BF16) for out, inverse in outs]
    blocks = n // step
    result = []
    for i in range(len(packs)):
        heads = []
        for h in range(HEADS):
            at = (i * HEADS + h) * blocks
            cols = outs[at : at + blocks]
            heads.append(cols[0] if blocks == 1 else jnp.concatenate(cols, axis=1))
        result.append(jnp.concatenate(heads, axis=0))
    return result


def gelu_pair(x):
    bell = jnp.exp2(x * x * (-0.5 * LOG2E))
    cdf = 0.5 + 0.5 * lax.erf(x * math.sqrt(0.5))
    return x * cdf, cdf + x * bell * (1.0 / math.sqrt(2.0 * math.pi))


def remote(src, dst, send, recv, device):
    return pltpu.make_async_remote_copy(
        src_ref=src,
        dst_ref=dst,
        send_sem=send,
        recv_sem=recv,
        device_id=device,
        device_id_type=pl.DeviceIdType.MESH,
    )


def loop(least, most, body):
    def run(k, carry):
        body(k)
        return carry

    lax.fori_loop(least, most, run, 0)


def layer_kernel(plan, *refs):
    (tl_ref, fl_ref, x_hbm, c_hbm, fw_ref, fp_ref, rw_ref, rp_ref, wi_ref, wo_ref, o_hbm, gi_ref, go_ref) = refs[:13]
    (x_ref, c_ref, o_ref, fwt_ref, fpt_ref, rwt_ref, lo_ref, hi_ref) = refs[13:21]
    (sl, sh, rl, rh, bs, nb, clo, chi, ai_ref, ao_ref, sb, r1, s1, r2) = refs[21:35]
    (x_sem, c_sem, o_sem, sl_sem, rl_sem, sh_sem, rh_sem, bs_sem, nb_sem, pair_sem, s2_sem, r2_sem) = refs[35:]
    rows, width, feats, groups, tables, factor = plan
    high = width - 128
    half = feats // 2
    npair = -(-half // groups)
    full = npair * groups
    nc, nc2 = rows // 8, rows // 16
    devices = groups * tables
    me = lax.axis_index("cells")
    table = lax.axis_index("tables")
    core = lax.rem(me, 2)
    sibling = me + 1 - 2 * core
    lane = lax.broadcasted_iota(jnp.int32, (half, 128), 1)

    def load_x(c):
        at = pl.ds(c * 8, 8)
        return pltpu.make_async_copy(x_hbm.at[at], x_ref.at[at], x_sem.at[c])

    def load_c():
        return pltpu.make_async_copy(c_hbm, c_ref, c_sem)

    def store_o(c):
        at = pl.ds(c * 8, 8)
        return pltpu.make_async_copy(o_ref.at[at], o_hbm.at[at], o_sem.at[c])

    def peer(k):
        return lax.rem(me + k, groups)

    def send_lo(c, k):
        p = peer(k)
        return remote(sl.at[c, p], rl.at[me, c], sl_sem.at[c, p], rl_sem.at[me, c], {"cells": p})

    def got_lo(c, k):
        p = peer(k)
        return remote(sl.at[c, p], rl.at[p, c], sl_sem.at[c, p], rl_sem.at[p, c], {"cells": p})

    def send_hi(c, k):
        p = peer(k)
        return remote(sh.at[c, p], rh.at[me, c], sh_sem.at[c, p], rh_sem.at[me, c], {"cells": p})

    def got_hi(c, k):
        p = peer(k)
        return remote(sh.at[c, p], rh.at[p, c], sh_sem.at[c, p], rh_sem.at[p, c], {"cells": p})

    def send_back(j, k):
        p = peer(k)
        return remote(bs.at[j, p], nb.at[me, j], bs_sem.at[j, p], nb_sem.at[me, j], {"cells": p})

    def got_back(j, p):
        return remote(bs.at[j, p], nb.at[p, j], bs_sem.at[j, p], nb_sem.at[p, j], {"cells": p})

    loop(0, nc, lambda c: load_x(c).start())
    load_c().start()

    barrier = pltpu.get_barrier_semaphore()

    def greet(k):
        d = lax.rem(table * groups + me + k, devices)
        device = {"tables": lax.div(d, groups), "cells": lax.rem(d, groups)}
        pl.semaphore_signal(barrier, inc=1, device_id=device, device_id_type=pl.DeviceIdType.MESH)

    loop(1, devices, greet)
    fwt_ref[...] = fw_ref[...].T
    fpt_ref[...] = fp_ref[...].T
    rwt_ref[...] = rw_ref[...].T

    flimit = fl_ref[0]
    if full > half:
        for ref in (lo_ref, hi_ref):
            ref[half * 16 :, :] = jnp.zeros(((full - half) * 16, 128), F32)

    def feature_step(c):
        load_x(c).wait()
        cells = [x_ref[c * 8 + k] for k in range(8)]
        packs = [dot(fwt_ref[...], x, 1, 0).astype(BF16) for x in cells]
        attended = attend(packs, flimit, feats, feats // 4)
        mixed = [dot(fpt_ref[...], a, 1, 0) for a in attended]
        for k in range(8):
            y = layer_norm(cells[k].astype(F32) + mixed[k], 0)
            yl = y[:128].T
            lo_ref[pl.ds(k, half, stride=16), :] = yl[:half]
            lo_ref[pl.ds(8 + k, half, stride=16), :] = yl[half:]
            yh = jnp.concatenate([y[128:], y[128:]], axis=0).T
            hi_ref[pl.ds(lax.rem(c, 2) * 8 + k, half, stride=16), :] = jnp.where(lane < high, yh[:half], yh[half:])

        sl[c] = lo_ref[...].astype(BF16).reshape(groups, npair, 16, 128)
        rl[me, c] = sl[c, me]

        @pl.when(c == 0)
        def _():
            pl.semaphore_wait(barrier, devices - 1)

        loop(1, groups, lambda k: send_lo(c, k).start())

        @pl.when(lax.rem(c, 2) == 1)
        def _():
            c2 = lax.div(c, 2)
            sh[c2] = hi_ref[...].astype(BF16).reshape(groups, npair, 16, 128)
            rh[me, c2] = sh[c2, me]
            loop(1, groups, lambda k: send_hi(c2, k).start())

    loop(0, nc, feature_step)

    load_c().wait()
    if full > half:
        for ref in (clo, chi):
            for at in (half, full + half):
                ref[at * rows : (at + full - half) * rows, :] = jnp.zeros(((full - half) * rows, 128), F32)

    def spread_rows(ref, r, value):
        if full == half:
            ref[pl.ds(r, feats, stride=rows), :] = value
        else:
            ref[pl.ds(r, half, stride=rows), :] = value[:half]
            ref[pl.ds(full * rows + r, half, stride=rows), :] = value[half:]

    def collect_rows(ref, r):
        if full == half:
            return ref[pl.ds(r, feats, stride=rows), :]
        spots = (pl.ds(r, half, stride=rows), pl.ds(full * rows + r, half, stride=rows))
        return jnp.concatenate([ref[spot, :] for spot in spots], axis=0)

    def cot_step(i):
        for k in range(4):
            r = i * 4 + k
            c = c_ref[r].astype(F32)
            spread_rows(clo, r, c[:128].T)
            spread_rows(chi, r, jnp.concatenate([c[128:], c[128:]], axis=0).T)

    loop(0, rows // 4, cot_step)

    def take(k):
        loop(0, nc, lambda c: got_lo(c, k).wait_recv())
        loop(0, nc2, lambda c: got_hi(c, k).wait_recv())

    loop(1, groups, take)

    tlimit = tl_ref[0]
    n = groups * rows
    pairs = 2 if npair % 2 == 0 and n <= 128 else 1

    def row_step(i):
        cells = []
        for k in range(pairs):
            j = i * pairs + k
            lo = rl[:, :, j].astype(F32).reshape(groups * nc, 2, 8, 128)
            hi = rh[:, :, j].reshape(n, 128)
            for f in range(2):
                part = lo[:, f].reshape(n, 128).astype(BF16)
                cells.append(jnp.concatenate([part, hi[:, f * high : (f + 1) * high]], axis=1))
        packs = [dot(rwt_ref[...], x, 1, 1).astype(BF16) for x in cells]
        attended = attend(packs, tlimit, n - n // 4, n // 4)
        mixed = [dot(a, rp_ref[...], 0, 0) for a in attended]
        done = [layer_norm(x.astype(F32) + m, -1) for x, m in zip(cells, mixed)]
        for k in range(pairs):
            j = i * pairs + k
            y0, y1 = done[2 * k], done[2 * k + 1]
            bs[j, :, 0] = y0[:, :128].astype(BF16).reshape(groups, rows, 128)
            bs[j, :, 1] = y1[:, :128].astype(BF16).reshape(groups, rows, 128)
            hi = jnp.concatenate([y0[:, 128:], y1[:, 128:]], axis=1)
            bs[j, :, 2] = hi.astype(BF16).reshape(groups, rows, 128)
        for k in range(pairs):
            j = i * pairs + k
            nb[me, j] = bs[j, me]
            loop(1, groups, lambda q: send_back(j, q).start())

    loop(0, npair // pairs, row_step)

    ai_ref[...] = jnp.zeros_like(ai_ref)
    ao_ref[...] = jnp.zeros_like(ao_ref)
    dp = divisor(npair, max(1, 256 // rows))
    steps = npair // dp
    span = dp * rows

    def dense_step(s):
        k = lax.div(s, steps)
        j0 = lax.rem(s, steps) * dp
        chip = lax.rem(me - core + 2 * lax.div(k, 2), groups)
        p = chip + lax.rem(core + k, 2)

        @pl.when(k > 0)
        def _():
            loop(0, dp, lambda j: got_back(j0 + j, p).wait_recv())

        block = nb[p, pl.ds(j0, dp)]
        hi = block[:, 2].reshape(span, 128)
        lo = jnp.concatenate([block[:, 0].reshape(span, 128), block[:, 1].reshape(span, 128)], axis=0)
        normed = jnp.concatenate([lo, jnp.concatenate([hi[:, :high], hi[:, high:]], axis=0)], axis=1)
        at0 = pl.ds((p * npair + j0) * rows, span)
        at1 = pl.ds((p * npair + j0 + full) * rows, span)
        clow = jnp.concatenate([clo[at0, :], clo[at1, :]], axis=0)
        chigh = jnp.concatenate([chi[at0, :], chi[at1, :]], axis=0)
        cot = jnp.concatenate([clow, chigh[:, :high]], axis=1).astype(BF16)
        act, slope = gelu_pair(dot(normed, wi_ref[...], 1, 0))
        act = act.astype(BF16)
        dpre = (dot(cot, wo_ref[...], 1, 0) * slope).astype(BF16)
        out = normed.astype(F32) + dot(act, wo_ref[...], 1, 1)
        clo[at0, :] = out[:span, :128]
        clo[at1, :] = out[span:, :128]
        chi[at0, :high] = out[:span, 128:]
        chi[at1, :high] = out[span:, 128:]
        ai_ref[...] += dot(normed, dpre, 0, 0)
        ao_ref[...] += dot(cot, act, 0, 0)

    loop(0, groups * steps, dense_step)

    def out_step(i):
        for k in range(4):
            r = i * 4 + k
            yl = collect_rows(clo, r).T
            yh = collect_rows(chi, r).T
            o_ref[r] = jnp.concatenate([yl, yh[:high]], axis=0).astype(BF16)

        @pl.when(lax.rem(i, 2) == 1)
        def _():
            store_o(lax.div(i, 2)).start()

    hidden = ai_ref.shape[1]
    own = hidden // devices
    if own % 8 == 0:
        n2, per = devices // 2, groups // 2
        myq = table * per + lax.div(me, 2)
        pad = sb.shape[2] - 3 * own

        def swap():
            return remote(sb.at[1 - core], r1, pair_sem.at[0], pair_sem.at[1], {"cells": sibling})

        def spread(k):
            q = lax.rem(myq + k, n2)
            device = {"tables": lax.div(q, per), "cells": lax.rem(q, per) * 2 + core}
            return remote(s1.at[q], r2.at[myq], s2_sem.at[q], r2_sem.at[myq], device)

        def gather(k):
            q = lax.rem(myq + k, n2)
            device = {"tables": lax.div(q, per), "cells": lax.rem(q, per) * 2 + core}
            return remote(s1.at[q], r2.at[q], s2_sem.at[q], r2_sem.at[q], device)

        gl = (ai_ref[:128] * factor).T.reshape(n2, 2, own, 128)
        go = (ao_ref[:128] * factor).T.reshape(n2, 2, own, 128)
        gh = (jnp.concatenate([ai_ref[128:], ao_ref[128:]], axis=0) * factor).T.reshape(n2, 2, own, 128)
        parts = [gl, go, gh] + ([gh[:, :, :pad]] if pad else [])
        sends = jnp.concatenate(parts, axis=2).astype(BF16)
        sb[0] = sends[:, 0]
        sb[1] = sends[:, 1]
        swap().start()
        loop(0, rows // 16, out_step)
        swap().wait()
        s1[...] = (sb[core].astype(F32) + r1[...].astype(F32)).astype(BF16)
        r2[myq] = s1[myq]
        loop(1, n2, lambda k: spread(k).start())
        loop(rows // 16, rows // 4, out_step)
        loop(1, n2, lambda k: gather(k).wait())
        total = jnp.sum(r2[...].astype(F32), axis=0)
        gh = total[2 * own : 3 * own]
        gi_ref[...] = jnp.concatenate([total[:own], gh[:, :high]], axis=1)
        go_ref[...] = jnp.concatenate([total[own : 2 * own], gh[:, high:]], axis=1)
    else:
        gi_ref[...] = (ai_ref[...] * factor).T.astype(BF16)
        go_ref[...] = (ao_ref[...] * factor).T.astype(BF16)
        loop(0, rows // 4, out_step)

    loop(0, nc, lambda c: store_o(c).wait())

    def drain(k):
        loop(0, nc, lambda c: send_lo(c, k).wait_send())
        loop(0, nc2, lambda c: send_hi(c, k).wait_send())
        loop(0, npair, lambda j: send_back(j, k).wait_send())

    loop(1, groups, drain)


def divisor(n, most):
    return max(k for k in range(1, most + 1) if n % k == 0)


def run_layer(factor, limits, x, cot, f_qkv, f_proj, r_qkv, r_proj, w_in, w_out):
    rows, width, feats = x.shape
    hidden = w_in.shape[1]
    groups, tables = lax.axis_size("cells"), lax.axis_size("tables")
    devices = groups * tables
    own = hidden // devices
    half = feats // 2
    npair = -(-half // groups)
    full = npair * groups
    nc, nc2, n2 = rows // 8, rows // 16, devices // 2
    direct = own % 8 == 0
    tall = -(-3 * own // 16) * 16 if direct else 16
    many = n2 if direct else 1
    grad = jax.ShapeDtypeStruct((own, width), F32) if direct else jax.ShapeDtypeStruct((hidden, width), BF16)
    smem = pl.BlockSpec(memory_space=pltpu.SMEM)
    far = pl.BlockSpec(memory_space=pl.ANY)
    near = pl.BlockSpec(memory_space=pltpu.VMEM)
    dma = pltpu.SemaphoreType.DMA
    cells = 2 * full * rows
    plan = (rows, width, feats, groups, tables, factor)
    return pl.pallas_call(
        lambda *refs: layer_kernel(plan, *refs),
        out_shape=[jax.ShapeDtypeStruct((rows, width, feats), BF16), grad, grad],
        in_specs=[smem, smem, far, far] + [near] * 6,
        out_specs=[far, near, near],
        scratch_shapes=[
            pltpu.VMEM((rows, width, feats), BF16),
            pltpu.VMEM((rows, width, feats), BF16),
            pltpu.VMEM((rows, width, feats), BF16),
            pltpu.VMEM(f_qkv.shape[::-1], BF16),
            pltpu.VMEM(f_proj.shape[::-1], BF16),
            pltpu.VMEM(r_qkv.shape[::-1], BF16),
            pltpu.VMEM((full * 16, 128), F32),
            pltpu.VMEM((full * 16, 128), F32),
            pltpu.VMEM((nc, groups, npair, 16, 128), BF16),
            pltpu.VMEM((nc2, groups, npair, 16, 128), BF16),
            pltpu.VMEM((groups, nc, npair, 16, 128), BF16),
            pltpu.VMEM((groups, nc2, npair, 16, 128), BF16),
            pltpu.VMEM((npair, groups, 3, rows, 128), BF16),
            pltpu.VMEM((groups, npair, 3, rows, 128), BF16),
            pltpu.VMEM((cells, 128), F32),
            pltpu.VMEM((cells, 128), F32),
            pltpu.VMEM((width, hidden), F32),
            pltpu.VMEM((width, hidden), F32),
            pltpu.VMEM((2, many, tall, 128), BF16),
            pltpu.VMEM((many, tall, 128), BF16),
            pltpu.VMEM((many, tall, 128), BF16),
            pltpu.VMEM((many, tall, 128), BF16),
            dma((nc,)),
            dma,
            dma((nc,)),
            dma((nc, groups)),
            dma((groups, nc)),
            dma((nc2, groups)),
            dma((groups, nc2)),
            dma((npair, groups)),
            dma((groups, npair)),
            dma((2,)),
            dma((many,)),
            dma((many,)),
        ],
        compiler_params=pltpu.CompilerParams(collective_id=0, has_side_effects=True),
        name="layer",
    )(*limits, x, cot, f_qkv, f_proj, r_qkv, r_proj, w_in, w_out)


def exchange_kernel(axes, sizes, x_ref, o_ref, own_ref, own_sem, send_sem, recv_sem):
    count = math.prod(sizes)
    me = 0
    for axis, size in zip(axes, sizes):
        me = me * size + lax.axis_index(axis)

    def target(k):
        peer = lax.rem(me + k, count)
        if len(axes) == 1:
            return peer, {axes[0]: peer}
        return peer, {axes[0]: lax.div(peer, sizes[1]), axes[1]: lax.rem(peer, sizes[1])}

    def copy(k):
        peer, device = target(k)
        return pltpu.make_async_remote_copy(
            src_ref=x_ref.at[peer],
            dst_ref=o_ref.at[me],
            send_sem=send_sem.at[k],
            recv_sem=recv_sem.at[k],
            device_id=device,
            device_id_type=pl.DeviceIdType.MESH,
        )

    barrier = pltpu.get_barrier_semaphore()

    def greet(k, carry):
        pl.semaphore_signal(barrier, inc=1, device_id=target(k)[1], device_id_type=pl.DeviceIdType.MESH)
        return carry

    def start(k, carry):
        copy(k).start()
        return carry

    def finish(k, carry):
        copy(k).wait()
        return carry

    load = pltpu.make_async_copy(x_ref.at[me], own_ref, own_sem.at[0])
    load.start()
    lax.fori_loop(1, count, greet, 0)
    pl.semaphore_wait(barrier, count - 1)
    lax.fori_loop(1, count, start, 0)
    load.wait()
    store = pltpu.make_async_copy(own_ref, o_ref.at[me], own_sem.at[1])
    store.start()
    lax.fori_loop(1, count, finish, 0)
    store.wait()


def exchange(array, axes, ident):
    sizes = [lax.axis_size(axis) for axis in axes]
    return pl.pallas_call(
        lambda *refs: exchange_kernel(axes, sizes, *refs),
        out_shape=jax.ShapeDtypeStruct(array.shape, array.dtype),
        in_specs=[pl.BlockSpec(memory_space=pl.ANY)],
        out_specs=pl.BlockSpec(memory_space=pl.ANY),
        scratch_shapes=[
            pltpu.VMEM(array.shape[1:], array.dtype),
            pltpu.SemaphoreType.DMA((2,)),
            pltpu.SemaphoreType.DMA((array.shape[0],)),
            pltpu.SemaphoreType.DMA((array.shape[0],)),
        ],
        compiler_params=pltpu.CompilerParams(collective_id=ident, has_side_effects=True),
        name="exchange%d" % ident,
    )(array)


def per_device(
    cells_in, train_count, feat_count, feat_qkv, feat_proj, row_qkv, row_proj, w_in, w_out, cotangent
):
    block = cells_in[0]
    rows, feats, width = block.shape
    devices = lax.axis_size("cells") * lax.axis_size("tables")
    factor = 1.0 / math.sqrt(devices * rows * feats)
    output, part_in, part_out = run_layer(
        factor,
        (train_count, feat_count),
        jnp.swapaxes(block, 1, 2),
        jnp.swapaxes(cotangent[0], 1, 2),
        feat_qkv,
        feat_proj,
        row_qkv,
        row_proj,
        w_in,
        w_out.T,
    )
    own = w_in.shape[1] // devices
    if part_in.shape[0] == own:
        return jnp.swapaxes(output, 1, 2)[None], part_in.T, part_out
    sends = jnp.concatenate([part_in.reshape(devices, own, width), part_out.reshape(devices, own, width)], axis=1)
    got = exchange(sends, AXES, 2)
    total = jnp.sum(got.astype(F32), axis=0)
    return jnp.swapaxes(output, 1, 2)[None], total[:own].T, total[own:]


def solution(mesh):
    return jax.shard_map(
        per_device,
        mesh=mesh,
        in_specs=(
            P("tables", "cells", None, None),
            P("tables"),
            P("tables"),
            P(),
            P(),
            P(),
            P(),
            P(),
            P(),
            P("tables", "cells", None, None),
        ),
        out_specs=(
            P("tables", "cells", None, None),
            P(None, ("tables", "cells")),
            P(("tables", "cells"), None),
        ),
        check_vma=False,
    )
```

time: 116 us -> 64.6 us (0.56)
  Pallas kernels: 109 us -> 58.6 us
  other arithmetic: 3.41 us -> 0 us
  local copies, waits for them, and re-layouts: 0.62 us -> 3.89 us
    pallas_call x6 -> x1, Pallas kernels: 109 us -> 58.6 us  [run_layer(): pl.pallas_call(lambda *refs: layer_kernel(plan, *refs), out_shape=[jax.Sh...]
    unnamed x0 -> x7, local copies, waits for them, and re-layouts: none -> 3.89 us
    concatenate x1 -> x0, other arithmetic: 2.13 us -> none  [per_device(): jnp.concatenate([part_in.reshape(devices, own, width), part_out.reshape(d...]
    reduce_sum x1 -> x0, other arithmetic: 1.28 us -> none  [per_device(): total = jnp.sum(got.astype(F32), axis=0)]
where the time goes in v1:
time: 64.6 us; the launch traced here: 64.4 us
  Pallas kernels  58.6 us (91%)
  local copies, waits for them, and re-layouts  3.89 us (6%)
  between operations  1.95 us (3%)
    pallas_call x1, Pallas kernels, run_layer(): pl.pallas_call(lambda *refs: layer_kernel(plan, *refs), out_shape=[jax.Sh...  58.6 us
    unnamed x7, local copies, waits for them, and re-layouts  3.89 us

profile of v1, /device:TPU:8, one launch (start us, length us, event | category | flops | bytes accessed | tf_op | source)
XLA Modules:
  0.0 64.4 jit_solution(1866352859364504208)
XLA Ops:
  1.9 58.6 %layer.1 = (bf16[32,192,112]{2,1,0:T(8,128)(2,1)}, f32[24,192]{1,0:T(8,128)}, f32[24,192]{1,0:T(8,128)}) custom-call(s32[1]{0:T(128)S(6)} %copy.16.refs_0_, s32[1]{0:T(128)S(6)} %copy.17.refs_1_, bf16[32,192,112]{2,1,0:T(8,128)(2,1)} %bitcast.11, bf16[32,192,112]{2,1,0:T(8,128)(2,1)} %bitcast.12, bf16[192,576]{1,0:T(8,128)(2,1)} %refs_4_.1, ...), custom_call_target="tpu_custom_call" | custom-call | tf_op jit(solution)/shard_map/layer/pallas_call | solution.py:388
  60.5 0.0 copy-start.1
  60.5 0.0 copy-start
  60.5 2.7 %copy.18 = bf16[1,32,112,192]{2,3,1,0:T(8,128)(2,1)} copy(bf16[1,32,112,192]{2,3,1,0:T(8,128)(2,1)} %bitcast.13) | data formatting | bytes 2752512
  63.2 0.0 copy-done.1
  63.2 0.6 copy.19
  63.8 0.0 copy-done
  63.8 0.6 copy.20
Async XLA Ops:
  60.5 2.7 %copy-start.1 = (f32[24,192]{1,0:T(8,128)S(1)}, f32[24,192]{1,0:T(8,128)}, u32[]{:S(2)}) copy-start(f32[24,192]{1,0:T(8,128)} %get-tuple-element.7) | copy-start | bytes 55300
  60.5 3.3 %copy-start = (f32[24,192]{1,0:T(8,128)S(1)}, f32[24,192]{1,0:T(8,128)}, u32[]{:S(2)}) copy-start(f32[24,192]{1,0:T(8,128)} %get-tuple-element.14) | copy-start | bytes 55300
